TPU v7x, 256 devices: a whole 4x4x8 slice. The times are simulated.
256 devices in a mesh: lon: 16 (over y_hi, z), day: 16 (over x, y_lo, core).
Axes of the slice: x: 4, y: 4 (y_hi: 2, y_lo: 2; y = y_hi * 2 + y_lo), z: 8, core: 2. Of those that a mesh axis runs over, the one named last changes fastest.
Arguments:
- field: bfloat16 [368, 1440, 1024], P('day', 'lon'), may hold values from -6 to 6
Outputs:
- filtered: float32 [368, 1440, 1024], P('day', 'lon')
All inputs are finite; a program needn't handle non-finite values.
Results may differ from a plain program's by a relative error of at most 0.0003.
Values may be sent and summed in bfloat16 or wider, within the bound.
A program may use at most 192 MiB of HBM per device.

v0:
```python
import functools

import jax
import jax.numpy as jnp
from jax import lax
from jax.experimental import pallas as pl
from jax.experimental.pallas import tpu as pltpu
from jax.sharding import PartitionSpec as P

DAY_HALF = 15
LON_HALF = 10
ROWS = 8
PAD = 24
LEAD = 3
MESH = pl.DeviceIdType.MESH


def plan(lons):
    group = DAY_HALF % ROWS + 1
    depth = -(-LON_HALF // group) * group
    left = [(at, group) for at in range(0, depth, group)]
    right = [(lons - at - group, group) for at in range(0, depth, group)]
    edges = [piece for pair in zip(left, right) for piece in pair]
    middle = [
        (at, min(group, lons - depth - at)) for at in range(depth, lons - depth, group)
    ]
    return edges, middle


def grid(rows, cols):
    return (
        lax.broadcasted_iota(jnp.int32, (rows, cols), 0),
        lax.broadcasted_iota(jnp.int32, (rows, cols), 1),
    )


def ones(condition):
    return jnp.where(condition, 1.0, 0.0).astype(jnp.bfloat16)


def band(days, rows, shift):
    day, other = grid(days, rows)
    away = jnp.abs(day - other - shift)
    weight = jnp.where(away <= DAY_HALF, -1.0, 0.0)
    if shift == 0:
        weight = jnp.where(away == 0, 2.0 * DAY_HALF, weight)
    return weight.astype(jnp.bfloat16)


def stacked(days, shift, extra):
    row, other = grid(2 * PAD, 2 * ROWS)
    low = (row < days) & (other < DAY_HALF) & (jnp.abs(row - other - shift) <= DAY_HALF)
    away = jnp.abs(row - PAD - (ROWS + extra) - shift)
    high = (row >= PAD) & (row < PAD + days) & (other == DAY_HALF) & (away <= DAY_HALF)
    return jnp.where(low | high, -1.0, 0.0).astype(jnp.bfloat16)


def kernel(
    counts, x, out, own, before, after, rest_before, rest_after, pack_up, pack_down,
    anomaly, own_sem, day_send, day_recv, lon_send, lon_recv,
    day_ready, lon_ready,
):
    lons, days, cols = x.shape
    half = LON_HALF
    tail = days - DAY_HALF
    part = DAY_HALF - ROWS
    group = part + 1
    day_count, lon_count = counts
    day, lon = lax.axis_index("day"), lax.axis_index("lon")
    day_next = lax.rem(day + 1, day_count)
    day_back = lax.rem(day + day_count - 1, day_count)
    lon_next = lax.rem(lon + 1, lon_count)
    lon_back = lax.rem(lon + lon_count - 1, lon_count)
    edges, middle = plan(lons)
    order = edges + middle

    loads = []
    for n, (at, size) in enumerate(order):
        loads.append(
            pltpu.make_async_copy(
                x.at[pl.ds(at, size)], own.at[pl.ds(at, size)], own_sem.at[n]
            )
        )
        loads[-1].start()

    barrier = pltpu.get_barrier_semaphore()
    even = lax.rem(day, 2) == 0
    odd = jnp.logical_not(even)

    def tell(semaphore, axis, peers):
        for peer in peers:
            pl.semaphore_signal(
                semaphore, inc=1, device_id={axis: peer}, device_id_type=MESH
            )

    @pl.when(odd)
    def _():
        tell(barrier, "day", (day_next, day_back))

    @pl.when(even)
    def _():
        pl.semaphore_wait(barrier, 2)
        tell(day_ready, "day", (day_next, day_back))

    @pl.when(odd)
    def _():
        pl.semaphore_wait(day_ready, 2)
        tell(barrier, "lon", (lon_next, lon_back))

    swaps = [[] for _ in order]

    def swap(n, kind, up_src, up_dst, down_src, down_dst):
        for way, src, dst, peer in (
            (0, up_src, up_dst, day_next), (1, down_src, down_dst, day_back),
        ):
            copy = pltpu.make_async_remote_copy(
                src_ref=src,
                dst_ref=dst,
                send_sem=day_send.at[kind, way, n],
                recv_sem=day_recv.at[kind, way, n],
                device_id={"day": peer},
                device_id_type=MESH,
            )
            copy.start()
            swaps[n].append(copy)

    def whole(n):
        at, size = order[n]
        if size == group:
            rows = pl.ds(at, size)
            swap(
                n, 0,
                x.at[rows, pl.ds(tail, ROWS)], before.at[rows, pl.ds(0, ROWS)],
                x.at[rows, pl.ds(0, ROWS)], after.at[rows, pl.ds(0, ROWS)],
            )
        else:
            rows = pl.ds(at, size)
            swap(
                n, 0,
                x.at[rows, pl.ds(tail, DAY_HALF)], rest_before,
                x.at[rows, pl.ds(0, 2 * ROWS)], rest_after,
            )

    row, col = grid(2 * ROWS, days)
    first_day = jnp.where(row < ROWS, tail + ROWS, ROWS)
    place = jnp.where(row < ROWS, row, row - ROWS)
    keep = ones((place < part) & (col == first_day + place))

    def dot(weight, values):
        return jnp.dot(weight, values, preferred_element_type=jnp.float32)

    def pack(n):
        at, size = order[n]
        loads[n].wait()
        if size < group:
            return

        @pl.loop(0, part)
        def _(i):
            ride = ones((place == part) & (col == first_day + i))
            tile = dot(keep, own[at + i]) + dot(ride, own[at + part])
            tile = tile.astype(jnp.bfloat16)
            pack_up[at + i] = tile[:ROWS]
            pack_down[at + i] = tile[ROWS:]

    def packed(n):
        at, size = order[n]
        if size == group:
            rows = pl.ds(at, part)
            swap(
                n, 1,
                pack_up.at[rows], before.at[rows, pl.ds(ROWS, ROWS)],
                pack_down.at[rows], after.at[rows, pl.ds(ROWS, ROWS)],
            )

    own_band = band(days, days, 0)
    before_band = band(days, DAY_HALF, -DAY_HALF)
    after_band = band(days, 2 * ROWS, days)
    before_top = band(days, ROWS, -DAY_HALF)
    after_top = band(days, ROWS, days)

    def daily(n):
        at, size = order[n]
        for copy in swaps[n]:
            copy.wait_recv()
        if size < group:
            for i in range(size):
                anomaly[at + i + half] = (
                    dot(own_band, own[at + i])
                    + dot(before_band, rest_before[i])
                    + dot(after_band, rest_after[i])
                )
            return

        last = at + part
        anomaly[last + half] = (
            dot(own_band, own[last])
            + dot(before_top, before[last, pl.ds(0, ROWS)])
            + dot(after_top, after[last, pl.ds(0, ROWS)])
        )

        @pl.loop(0, part)
        def _(i):
            l = at + i
            both = dot(stacked(days, -DAY_HALF, i), before[l]) + dot(
                stacked(days, days, i), after[l]
            )
            anomaly[l + half] = dot(own_band, own[l]) + both[:days]
            anomaly[last + half] = anomaly[last + half] + both[PAD : PAD + days]

    def edge(n):
        at, size = order[n]
        low = n % 2 == 0
        if low:
            size = min(size, half - at)
            place = at + lons + half
        else:
            end = at + size
            at = max(at, lons - half)
            size = end - at
            place = at - lons + half
        side = 0 if low else 1
        copy = pltpu.make_async_remote_copy(
            src_ref=anomaly.at[pl.ds(at + half, size)],
            dst_ref=anomaly.at[pl.ds(place, size)],
            send_sem=lon_send.at[side, n],
            recv_sem=lon_recv.at[side, n],
            device_id={"lon": lon_back if low else lon_next},
            device_id_type=MESH,
        )
        copy.start()
        return copy

    steps = len(order)
    for n in range(LEAD):
        whole(n)
    for n in range(steps):
        pack(n)
        if n > 0:
            packed(n - 1)
    packed(steps - 1)
    for n in range(LEAD, steps):
        whole(n)
    shifts = []

    def advance(n):
        daily(n)
        if 0 < n <= len(edges):
            shifts.append(edge(n - 1))

    @pl.when(odd)
    def _():
        pl.semaphore_wait(barrier, 2)
        tell(lon_ready, "day", (day_back,))

    @pl.when(even)
    def _():
        pl.semaphore_wait(lon_ready, 1)

    for n in range(len(edges)):
        advance(n)

    scale = 1.0 / ((2 * DAY_HALF + 1) * (2 * half + 1))
    width = 2 * half + 1

    def up_to(lo, hi, total):
        def step(l, total):
            total = total + (anomaly[l + width - 1] - anomaly[l - 1])
            out[l] = total * scale
            return total

        return lax.fori_loop(lo, hi, step, total)

    def back(step, total):
        l = half - 1 - step
        total = total + (anomaly[l] - anomaly[l + width])
        out[l] = total * scale
        return total

    total = None
    done = half
    for n in range(len(edges), steps):
        end = n == steps - 1
        if end and total is not None:
            for copy in shifts:
                copy.wait_recv()
            lax.fori_loop(0, half, back, first)
        advance(n)
        ready = lons - half if end else sum(order[n]) - half
        if ready <= half:
            continue
        fresh = total is None
        if fresh:
            total = lax.fori_loop(
                half,
                half + width,
                lambda l, t: t + anomaly[l],
                jnp.zeros((days, cols), jnp.float32),
            )
            out[half] = total * scale
            first = total
            done = half + 1
        total = up_to(done, ready, total)
        done = ready
    up_to(done, lons, total)

    for copies in swaps:
        for copy in copies:
            copy.wait_send()
    for copy in shifts:
        copy.wait_send()


def local(counts, field):
    days, lons, cols = field.shape
    x = jnp.transpose(field, (1, 0, 2))
    edges, middle = plan(lons)
    steps = len(edges) + len(middle)
    rest = middle[-1][1]
    y = pl.pallas_call(
        functools.partial(kernel, counts),
        out_shape=pltpu.VMEM((lons, days, cols), jnp.float32),
        in_specs=[pl.BlockSpec(memory_space=pltpu.HBM)],
        out_specs=pl.BlockSpec(memory_space=pltpu.VMEM),
        scratch_shapes=[
            pltpu.VMEM((lons, days, cols), jnp.bfloat16),
            pltpu.VMEM((lons, 2 * ROWS, cols), jnp.bfloat16),
            pltpu.VMEM((lons, 2 * ROWS, cols), jnp.bfloat16),
            pltpu.VMEM((rest, DAY_HALF, cols), jnp.bfloat16),
            pltpu.VMEM((rest, 2 * ROWS, cols), jnp.bfloat16),
            pltpu.VMEM((lons, ROWS, cols), jnp.bfloat16),
            pltpu.VMEM((lons, ROWS, cols), jnp.bfloat16),
            pltpu.VMEM((lons + 2 * LON_HALF, days, cols), jnp.float32),
            pltpu.SemaphoreType.DMA((steps,)),
            pltpu.SemaphoreType.DMA((2, 2, steps)),
            pltpu.SemaphoreType.DMA((2, 2, steps)),
            pltpu.SemaphoreType.DMA((2, len(edges))),
            pltpu.SemaphoreType.DMA((2, len(edges))),
            pltpu.SemaphoreType.REGULAR,
            pltpu.SemaphoreType.REGULAR,
        ],
        compiler_params=pltpu.CompilerParams(
            collective_id=0, has_side_effects=True, vmem_limit_bytes=50 * 1024 * 1024
        ),
    )(x)
    return jnp.transpose(y, (1, 0, 2))


def solution(mesh):
    return jax.shard_map(
        functools.partial(local, (mesh.shape["day"], mesh.shape["lon"])),
        mesh=mesh,
        in_specs=(P("day", "lon", None),),
        out_specs=P("day", "lon", None),
        check_vma=False,
    )
```

profile of v0, /device:TPU:1, one launch (start us, length us, event | category | flops | bytes accessed | tf_op | source)
XLA Modules:
  0.0 94.2 jit_solution(1330426719420351403)
XLA Ops:
  0.0 90.7 %shard_map.17 = f32[90,23,1024]{2,1,0:T(8,128)S(1)} custom-call(bf16[90,23,1024]{2,1,0:T(8,128)(2,1)} %bitcast.3), custom_call_target="tpu_custom_call" | custom-call | tf_op jit(solution)/shard_map/pallas_call | solution.py:320
  90.7 3.6 %copy.3 = f32[23,90,1024]{2,0,1:T(8,128)} copy(f32[23,90,1024]{2,0,1:T(8,128)S(1)} %bitcast.2) | data formatting | bytes 16957440
where the time goes:
time: 94.5 us; the launch traced here: 94.2 us
  Pallas kernels  90.7 us (96%)
  local copies, waits for them, and re-layouts  3.55 us (4%)
    pallas_call x1, Pallas kernels, local(): pl.pallas_call(functools.partial(kernel, counts), out_shape=pltpu.VMEM((l...  90.7 us
    unnamed x1, local copies, waits for them, and re-layouts  3.55 us

commit v1 on v0

v1 whole, which is shorter than its diff:
```python
import functools

import jax
import jax.numpy as jnp
from jax import lax
from jax.experimental import pallas as pl
from jax.experimental.pallas import tpu as pltpu
from jax.sharding import PartitionSpec as P

DAY_HALF = 15
LON_HALF = 10
ROWS = 8
RUN = 8
BLOCK = 10
MESH = pl.DeviceIdType.MESH


def plan(lons):
    edges = [
        (0, ROWS, ROWS - 1),
        (lons - ROWS, ROWS, lons - ROWS),
        (ROWS, ROWS, 2 * ROWS - 1),
        (lons - 2 * ROWS, ROWS, lons - 2 * ROWS),
    ]
    middle = []
    for at in range(2 * ROWS, lons - 2 * ROWS, ROWS):
        size = min(ROWS, lons - 2 * ROWS - at)
        middle.append((at, size, at + ROWS - 1 if size == ROWS else None))
    return edges, middle


def hosts(group):
    at, size, rider = group
    if rider is None:
        return at, size
    return (at, size - 1) if rider > at else (at + 1, size - 1)


def grid(rows, cols):
    return (
        lax.broadcasted_iota(jnp.int32, (rows, cols), 0),
        lax.broadcasted_iota(jnp.int32, (rows, cols), 1),
    )


def ones(condition):
    return jnp.where(condition, 1.0, 0.0).astype(jnp.bfloat16)


def band(days, rows, shift):
    day, other = grid(days, rows)
    away = jnp.abs(day - other - shift)
    weight = jnp.where(away <= DAY_HALF, -1.0, 0.0)
    if shift == 0:
        weight = jnp.where(away == 0, 2.0 * DAY_HALF, weight)
    return weight.astype(jnp.bfloat16)


def dot(weight, values):
    return jnp.dot(weight, values, preferred_element_type=jnp.float32)


def kernel(
    counts, x, out, own, far_days, after, before, packed, anomaly,
    edge_own, edge_before, edge_after,
    own_sem, far_send, far_recv, near_send, near_recv, lon_send, lon_recv,
    jump_send, jump_recv, jump_ready,
):
    lons, days, cols = x.shape
    half = LON_HALF
    day_count, lon_count = counts
    day, lon = lax.axis_index("day"), lax.axis_index("lon")
    day_next = lax.rem(day + 1, day_count)
    day_back = lax.rem(day + day_count - 1, day_count)
    lon_next = lax.rem(lon + 1, lon_count)
    lon_back = lax.rem(lon + lon_count - 1, lon_count)
    even = lax.rem(day, 2) == 0
    odd = jnp.logical_not(even)
    far = jnp.where(even, day_back, day_next)
    near = jnp.where(even, day_next, day_back)
    low_jump = lax.rem(lon, RUN) == 0
    high_jump = lax.rem(lon, RUN) == RUN - 1
    jump = jnp.logical_or(low_jump, high_jump)
    peer = jnp.where(high_jump, lon_next, lon_back)
    edges, middle = plan(lons)
    order = edges + middle
    blocks = lons // BLOCK

    def load(b):
        rows = pl.ds(b * BLOCK, BLOCK)
        return pltpu.make_async_copy(x.at[rows], own.at[rows], own_sem.at[b])

    sequence = [0, blocks - 1, 1, blocks - 2, *range(2, blocks - 2)]
    for b in sequence:
        load(b).start()

    barrier = pltpu.get_barrier_semaphore()
    for axis, who in (
        ("day", day_next), ("day", day_back), ("lon", lon_next), ("lon", lon_back),
    ):
        pl.semaphore_signal(barrier, inc=1, device_id={axis: who}, device_id_type=MESH)
    pl.semaphore_wait(barrier, 4)

    @pl.when(jump)
    def _():
        pl.semaphore_signal(
            jump_ready, inc=1, device_id={"day": far}, device_id_type=MESH
        )

    def remote(src, dst, send, recv, to):
        return pltpu.make_async_remote_copy(
            src_ref=src, dst_ref=dst, send_sem=send, recv_sem=recv,
            device_id=to, device_id_type=MESH,
        )

    start = pl.multiple_of(jnp.where(even, 0, ROWS), ROWS)

    def whole(n):
        at, size, _ = order[n]
        rows = pl.ds(at, size)
        return remote(
            x.at[rows, pl.ds(start, ROWS)], far_days.at[rows, pl.ds(0, ROWS)],
            far_send.at[0, n], far_recv.at[0, n], {"day": far},
        )

    def second(n):
        rows = pl.ds(*hosts(order[n]))
        return remote(
            packed.at[rows], far_days.at[rows, pl.ds(ROWS, ROWS)],
            far_send.at[1, n], far_recv.at[1, n], {"day": far},
        )

    def near_even(b):
        rows = pl.ds(b * BLOCK, BLOCK)
        return remote(
            x.at[rows, pl.ds(ROWS, DAY_HALF)], before.at[rows],
            near_send.at[b], near_recv.at[b], {"day": near},
        )

    def near_odd(b):
        rows = pl.ds(b * BLOCK, BLOCK)
        return remote(
            x.at[rows, pl.ds(0, 2 * ROWS)], after.at[rows],
            near_send.at[b], near_recv.at[b], {"day": near},
        )

    edge = pl.ds(jnp.where(high_jump, lons - half, 0), half)
    across = {"lon": peer}
    corner = {"day": far, "lon": peer}

    def jump_even():
        return [
            remote(x.at[edge, pl.ds(ROWS, DAY_HALF)], edge_own.at[:, pl.ds(ROWS, DAY_HALF)],
                   jump_send.at[0], jump_recv.at[0], across),
        ]

    def jump_odd():
        return [
            remote(x.at[edge, pl.ds(0, ROWS)], edge_own.at[:, pl.ds(0, ROWS)],
                   jump_send.at[0], jump_recv.at[0], across),
            remote(x.at[edge, pl.ds(2 * ROWS, days - 2 * ROWS)],
                   edge_own.at[:, pl.ds(2 * ROWS, days - 2 * ROWS)],
                   jump_send.at[1], jump_recv.at[1], across),
        ]

    def corner_even():
        return [
            remote(x.at[edge, pl.ds(0, 2 * ROWS)], edge_after,
                   jump_send.at[2], jump_recv.at[2], corner),
            remote(far_days.at[edge, pl.ds(0, ROWS)], edge_own.at[:, pl.ds(ROWS, ROWS)],
                   jump_send.at[3], jump_recv.at[3], corner),
        ]

    def corner_odd():
        return [
            remote(x.at[edge, pl.ds(ROWS, DAY_HALF)], edge_before,
                   jump_send.at[4], jump_recv.at[4], corner),
            remote(far_days.at[edge, pl.ds(0, ROWS)], edge_own.at[:, pl.ds(0, ROWS)],
                   jump_send.at[5], jump_recv.at[5], corner),
        ]

    def pass_even():
        return remote(edge_own.at[:, pl.ds(ROWS, DAY_HALF)], edge_before,
                      jump_send.at[6], jump_recv.at[6], {"day": near})

    def pass_odd():
        return remote(edge_own.at[:, pl.ds(0, 2 * ROWS)], edge_after,
                      jump_send.at[7], jump_recv.at[7], {"day": near})

    jump_is_even = jnp.logical_and(jump, even)
    jump_is_odd = jnp.logical_and(jump, odd)

    for n in range(len(edges)):
        whole(n).start()

    @pl.when(even)
    def _():
        for b in range(blocks):
            near_even(b).start()

    @pl.when(odd)
    def _():
        for b in range(blocks):
            near_odd(b).start()

    @pl.when(jump)
    def _():
        pl.semaphore_wait(jump_ready, 1)

    @pl.when(jump_is_even)
    def _():
        for copy in jump_even():
            copy.start()
        corner_even()[0].start()

    @pl.when(jump_is_odd)
    def _():
        for copy in jump_odd():
            copy.start()
        corner_odd()[0].start()

    place, col = grid(ROWS, days)
    part = DAY_HALF - ROWS
    first = jnp.where(even, ROWS, 2 * ROWS)
    keep = ones((place < part) & (col == first + place))

    def pack(n):
        at, size = hosts(order[n])
        rider = order[n][2]
        for i in range(size):
            tile = dot(keep, own[at + i])
            if rider is not None:
                ride = ones((place == part) & (col == first + i))
                tile = tile + dot(ride, own[rider])
            packed[at + i] = tile.astype(jnp.bfloat16)

    waited = 0
    for n in range(len(order)):
        at, size, _ = order[n]
        need = 2 if n < 2 else 4 if n < 4 else min(
            blocks, max(4, sequence.index(min((at + size - 1) // BLOCK, blocks - 3)) + 1)
        )
        while waited < need:
            load(sequence[waited]).wait()
            waited += 1
        if n >= len(edges):
            whole(n).start()
        pack(n)
        if n > 0:
            second(n - 1).start()
    while waited < blocks:
        load(sequence[waited]).wait()
        waited += 1
    own_band = band(3 * ROWS, days, 0)
    before_band = band(3 * ROWS, DAY_HALF, -DAY_HALF)
    after_band = band(3 * ROWS, 2 * ROWS, days)
    second(len(order) - 1).start()

    @pl.when(even)
    def _():
        @pl.loop(0, blocks)
        def _(b):
            near_odd(b).wait_recv()
            for i in range(BLOCK):
                l = b * BLOCK + i
                anomaly[l + half] = dot(own_band, own[l]) + dot(after_band, after[l])

    @pl.when(odd)
    def _():
        @pl.loop(0, blocks)
        def _(b):
            near_even(b).wait_recv()
            for i in range(BLOCK):
                l = b * BLOCK + i
                anomaly[l + half] = dot(own_band, own[l]) + dot(before_band, before[l])

    row, other = grid(2 * ROWS, 2 * ROWS)
    way = jnp.where(even, 1, -1)
    far_band = jnp.where(
        ((other - row) * way >= 0) & (other < DAY_HALF), -1.0, 0.0
    ).astype(jnp.bfloat16)
    touched = pl.ds(start, 2 * ROWS)
    lane, source = grid(ROWS, ROWS)

    def daily(n):
        at, size, rider = order[n]
        whole(n).wait_recv()
        second(n).wait_recv()
        if rider is not None:
            host, count = hosts(order[n])
            tile = jnp.zeros((ROWS, cols), jnp.float32)
            for i in range(count):
                take = ones((lane == i) & (source == part))
                tile = tile + dot(take, far_days[host + i, pl.ds(ROWS, ROWS)])
            far_days[rider, pl.ds(ROWS, ROWS)] = tile.astype(jnp.bfloat16)
        for l in range(at, at + size):
            anomaly[l + half, touched] += dot(far_band, far_days[l])

    pieces = [
        (0, ROWS), (lons - ROWS, ROWS), (ROWS, half - ROWS), (lons - half, half - ROWS),
    ]

    def shift(n):
        at, size = pieces[n]
        low = n % 2 == 0
        place = at + half + (lons if low else -lons)
        return remote(
            anomaly.at[pl.ds(at + half, size)], anomaly.at[pl.ds(place, size)],
            lon_send.at[n], lon_recv.at[n], {"lon": lon_back if low else lon_next},
        )

    def advance(n):
        daily(n)
        if 0 < n <= len(edges):
            stays = low_jump if (n - 1) % 2 == 0 else high_jump

            @pl.when(jnp.logical_not(stays))
            def _():
                shift(n - 1).start()

    for n in range(len(edges)):
        advance(n)

    @pl.when(jump_is_even)
    def _():
        corner_even()[1].start()

    @pl.when(jump_is_odd)
    def _():
        corner_odd()[1].start()

    def pass_on():
        @pl.when(jump_is_even)
        def _():
            jump_even()[0].wait_recv()
            corner_odd()[1].wait_recv()
            pass_even().start()

        @pl.when(jump_is_odd)
        def _():
            for copy in jump_odd():
                copy.wait_recv()
            corner_even()[1].wait_recv()
            pass_odd().start()

    def zonal_edges():
        @pl.when(jump)
        def _():
            @pl.when(even)
            def _():
                corner_odd()[0].wait_recv()
                pass_odd().wait_recv()

            @pl.when(odd)
            def _():
                corner_even()[0].wait_recv()
                pass_even().wait_recv()

            to = jnp.where(high_jump, lons + half, 0)
            for i in range(half):
                anomaly[to + i] = (
                    dot(own_band, edge_own[i])
                    + dot(before_band, edge_before[i])
                    + dot(after_band, edge_after[i])
                )

        @pl.when(jnp.logical_not(high_jump))
        def _():
            shift(0).wait_recv()
            shift(2).wait_recv()

        @pl.when(jnp.logical_not(low_jump))
        def _():
            shift(1).wait_recv()
            shift(3).wait_recv()

    scale = 1.0 / ((2 * DAY_HALF + 1) * (2 * half + 1))
    width = 2 * half + 1

    def up_to(lo, hi, total):
        def step(l, total):
            total = total + (anomaly[l + width - 1] - anomaly[l - 1])
            out[l] = (total * scale)[:days]
            return total

        return lax.fori_loop(lo, hi, step, total)

    def back(step, total):
        l = half - 1 - step
        total = total + (anomaly[l] - anomaly[l + width])
        out[l] = (total * scale)[:days]
        return total

    steps = len(order)
    total = None
    done = half
    for n in range(len(edges), steps):
        end = n == steps - 1
        if n == steps - 3:
            pass_on()
        if end:
            zonal_edges()
            lax.fori_loop(0, half, back, first_total)
        advance(n)
        ready = lons if end else order[n][0] + order[n][1] - half
        if ready <= half:
            continue
        if total is None:
            total = lax.fori_loop(
                half,
                half + width,
                lambda l, t: t + anomaly[l],
                jnp.zeros((3 * ROWS, cols), jnp.float32),
            )
            out[half] = (total * scale)[:days]
            first_total = total
            done = half + 1
        total = up_to(done, ready, total)
        done = ready

    for n in range(steps):
        whole(n).wait_send()
        second(n).wait_send()

    @pl.when(even)
    def _():
        for b in range(blocks):
            near_even(b).wait_send()

    @pl.when(odd)
    def _():
        for b in range(blocks):
            near_odd(b).wait_send()

    for n in range(len(pieces)):
        stays = low_jump if n % 2 == 0 else high_jump

        @pl.when(jnp.logical_not(stays))
        def _():
            shift(n).wait_send()

    @pl.when(jump_is_even)
    def _():
        for copy in (*jump_even(), *corner_even(), pass_even()):
            copy.wait_send()

    @pl.when(jump_is_odd)
    def _():
        for copy in (*jump_odd(), *corner_odd(), pass_odd()):
            copy.wait_send()


def local(counts, field):
    days, lons, cols = field.shape
    x = jnp.transpose(field, (1, 0, 2))
    edges, middle = plan(lons)
    steps = len(edges) + len(middle)
    half = LON_HALF
    y = pl.pallas_call(
        functools.partial(kernel, counts),
        out_shape=pltpu.VMEM((lons, days, cols), jnp.float32),
        in_specs=[pl.BlockSpec(memory_space=pltpu.HBM)],
        out_specs=pl.BlockSpec(memory_space=pltpu.VMEM),
        scratch_shapes=[
            pltpu.VMEM((lons, days, cols), jnp.bfloat16),
            pltpu.VMEM((lons, 2 * ROWS, cols), jnp.bfloat16),
            pltpu.VMEM((lons, 2 * ROWS, cols), jnp.bfloat16),
            pltpu.VMEM((lons, DAY_HALF, cols), jnp.bfloat16),
            pltpu.VMEM((lons, ROWS, cols), jnp.bfloat16),
            pltpu.VMEM((lons + 2 * half, 3 * ROWS, cols), jnp.float32),
            pltpu.VMEM((half, days, cols), jnp.bfloat16),
            pltpu.VMEM((half, DAY_HALF, cols), jnp.bfloat16),
            pltpu.VMEM((half, 2 * ROWS, cols), jnp.bfloat16),
            pltpu.SemaphoreType.DMA((lons // BLOCK,)),
            pltpu.SemaphoreType.DMA((2, steps)),
            pltpu.SemaphoreType.DMA((2, steps)),
            pltpu.SemaphoreType.DMA((lons // BLOCK,)),
            pltpu.SemaphoreType.DMA((lons // BLOCK,)),
            pltpu.SemaphoreType.DMA((4,)),
            pltpu.SemaphoreType.DMA((4,)),
            pltpu.SemaphoreType.DMA((8,)),
            pltpu.SemaphoreType.DMA((8,)),
            pltpu.SemaphoreType.REGULAR,
        ],
        compiler_params=pltpu.CompilerParams(
            collective_id=0, has_side_effects=True, vmem_limit_bytes=52 * 1024 * 1024
        ),
    )(x)
    return jnp.transpose(y, (1, 0, 2))


def solution(mesh):
    return jax.shard_map(
        functools.partial(local, (mesh.shape["day"], mesh.shape["lon"])),
        mesh=mesh,
        in_specs=(P("day", "lon", None),),
        out_specs=P("day", "lon", None),
        check_vma=False,
    )
```

time: 94.5 us -> 83.7 us (0.89)
  Pallas kernels: 90.7 us -> 80.1 us
    pallas_call x1, Pallas kernels: 90.7 us -> 80.1 us  [local(): pl.pallas_call(functools.partial(kernel, counts), out_shape=pltpu.VMEM((l...]
where the time goes in v1:
time: 83.7 us; the launch traced here: 83.6 us
  Pallas kernels  80.1 us (96%)
  local copies, waits for them, and re-layouts  3.55 us (4%)
    pallas_call x1, Pallas kernels, local(): pl.pallas_call(functools.partial(kernel, counts), out_shape=pltpu.VMEM((l...  80.1 us
    unnamed x1, local copies, waits for them, and re-layouts  3.55 us

profile of v1, /device:TPU:1, one launch (start us, length us, event | category | flops | bytes accessed | tf_op | source)
XLA Modules:
  0.0 83.6 jit_solution(16457397529190037058)
XLA Ops:
  0.0 80.1 %shard_map.17 = f32[90,23,1024]{2,1,0:T(8,128)S(1)} custom-call(bf16[90,23,1024]{2,1,0:T(8,128)(2,1)} %bitcast.3), custom_call_target="tpu_custom_call" | custom-call | tf_op jit(solution)/shard_map/pallas_call | solution.py:459
  80.1 3.6 %copy.3 = f32[23,90,1024]{2,0,1:T(8,128)} copy(f32[23,90,1024]{2,0,1:T(8,128)S(1)} %bitcast.2) | data formatting | bytes 16957440

commit v2 on v1

--- a/solution.py
+++ b/solution.py
@@ -62,9 +62,9 @@
 
 def kernel(
     counts, x, out, own, far_days, after, before, packed, anomaly,
-    edge_own, edge_before, edge_after,
+    edge_own, edge_before, edge_after, edge_pass, edge_pack,
     own_sem, far_send, far_recv, near_send, near_recv, lon_send, lon_recv,
-    jump_send, jump_recv, jump_ready,
+    jump_send, jump_recv, near_ready, far_ready, lon_ready,
 ):
     lons, days, cols = x.shape
     half = LON_HALF
@@ -95,17 +95,43 @@
         load(b).start()
 
     barrier = pltpu.get_barrier_semaphore()
-    for axis, who in (
-        ("day", day_next), ("day", day_back), ("lon", lon_next), ("lon", lon_back),
-    ):
-        pl.semaphore_signal(barrier, inc=1, device_id={axis: who}, device_id_type=MESH)
-    pl.semaphore_wait(barrier, 4)
-
-    @pl.when(jump)
-    def _():
-        pl.semaphore_signal(
-            jump_ready, inc=1, device_id={"day": far}, device_id_type=MESH
-        )
+    seat = lax.rem(day, 4)
+    hub = seat == 1
+    rest = jnp.logical_not(hub)
+
+    def tell(semaphore, axis, *peers):
+        for who in peers:
+            pl.semaphore_signal(
+                semaphore, inc=1, device_id={axis: who}, device_id_type=MESH
+            )
+
+    @pl.when(jnp.logical_or(hub, seat == 3))
+    def _():
+        tell(barrier, "day", day_back, day_next)
+
+    @pl.when(seat == 0)
+    def _():
+        tell(barrier, "day", day_back)
+
+    @pl.when(seat == 2)
+    def _():
+        tell(barrier, "day", day_next)
+
+    @pl.when(rest)
+    def _():
+        pl.semaphore_wait(barrier, 2)
+
+    @pl.when(seat == 0)
+    def _():
+        tell(near_ready, "day", day_next)
+
+    @pl.when(seat == 2)
+    def _():
+        tell(far_ready, "day", day_back)
+
+    @pl.when(hub)
+    def _():
+        pl.semaphore_wait(far_ready, 1)
 
     def remote(src, dst, send, recv, to):
         return pltpu.make_async_remote_copy(
@@ -149,25 +175,18 @@
     corner = {"day": far, "lon": peer}
 
     def jump_even():
-        return [
-            remote(x.at[edge, pl.ds(ROWS, DAY_HALF)], edge_own.at[:, pl.ds(ROWS, DAY_HALF)],
-                   jump_send.at[0], jump_recv.at[0], across),
-        ]
+        return remote(edge_pack, edge_own.at[:, pl.ds(2 * ROWS, ROWS)],
+                      jump_send.at[0], jump_recv.at[0], across)
 
     def jump_odd():
-        return [
-            remote(x.at[edge, pl.ds(0, ROWS)], edge_own.at[:, pl.ds(0, ROWS)],
-                   jump_send.at[0], jump_recv.at[0], across),
-            remote(x.at[edge, pl.ds(2 * ROWS, days - 2 * ROWS)],
-                   edge_own.at[:, pl.ds(2 * ROWS, days - 2 * ROWS)],
-                   jump_send.at[1], jump_recv.at[1], across),
-        ]
+        return remote(x.at[edge, pl.ds(0, ROWS)], edge_own.at[:, pl.ds(0, ROWS)],
+                      jump_send.at[0], jump_recv.at[0], across)
 
     def corner_even():
         return [
             remote(x.at[edge, pl.ds(0, 2 * ROWS)], edge_after,
                    jump_send.at[2], jump_recv.at[2], corner),
-            remote(far_days.at[edge, pl.ds(0, ROWS)], edge_own.at[:, pl.ds(ROWS, ROWS)],
+            remote(far_days.at[edge], edge_own.at[:, pl.ds(ROWS, 2 * ROWS)],
                    jump_send.at[3], jump_recv.at[3], corner),
         ]
 
@@ -175,12 +194,12 @@
         return [
             remote(x.at[edge, pl.ds(ROWS, DAY_HALF)], edge_before,
                    jump_send.at[4], jump_recv.at[4], corner),
-            remote(far_days.at[edge, pl.ds(0, ROWS)], edge_own.at[:, pl.ds(0, ROWS)],
+            remote(far_days.at[edge], edge_own.at[:, pl.ds(0, 2 * ROWS)],
                    jump_send.at[5], jump_recv.at[5], corner),
         ]
 
     def pass_even():
-        return remote(edge_own.at[:, pl.ds(ROWS, DAY_HALF)], edge_before,
+        return remote(edge_own.at[:, pl.ds(ROWS, 2 * ROWS)], edge_pass,
                       jump_send.at[6], jump_recv.at[6], {"day": near})
 
     def pass_odd():
@@ -193,6 +212,11 @@
     for n in range(len(edges)):
         whole(n).start()
 
+    @pl.when(hub)
+    def _():
+        pl.semaphore_wait(near_ready, 1)
+        tell(barrier, "lon", lon_back, lon_next)
+
     @pl.when(even)
     def _():
         for b in range(blocks):
@@ -202,22 +226,6 @@
     def _():
         for b in range(blocks):
             near_odd(b).start()
-
-    @pl.when(jump)
-    def _():
-        pl.semaphore_wait(jump_ready, 1)
-
-    @pl.when(jump_is_even)
-    def _():
-        for copy in jump_even():
-            copy.start()
-        corner_even()[0].start()
-
-    @pl.when(jump_is_odd)
-    def _():
-        for copy in jump_odd():
-            copy.start()
-        corner_odd()[0].start()
 
     place, col = grid(ROWS, days)
     part = DAY_HALF - ROWS
@@ -256,6 +264,12 @@
     after_band = band(3 * ROWS, 2 * ROWS, days)
     second(len(order) - 1).start()
 
+    @pl.when(jump_is_even)
+    def _():
+        take = ones(col == DAY_HALF + place)
+        for i in range(half):
+            edge_pack[i] = dot(take, own[edge.start + i]).astype(jnp.bfloat16)
+
     @pl.when(even)
     def _():
         @pl.loop(0, blocks)
@@ -273,6 +287,35 @@
             for i in range(BLOCK):
                 l = b * BLOCK + i
                 anomaly[l + half] = dot(own_band, own[l]) + dot(before_band, before[l])
+
+    @pl.when(hub)
+    def _():
+        pl.semaphore_wait(barrier, 2)
+        tell(lon_ready, "day", day_back, day_next)
+
+    @pl.when(seat == 0)
+    def _():
+        pl.semaphore_wait(lon_ready, 1)
+        tell(lon_ready, "day", day_back)
+
+    @pl.when(seat == 2)
+    def _():
+        pl.semaphore_wait(lon_ready, 1)
+        tell(lon_ready, "day", day_next)
+
+    @pl.when(seat == 3)
+    def _():
+        pl.semaphore_wait(lon_ready, 2)
+
+    @pl.when(jump_is_even)
+    def _():
+        jump_even().start()
+        corner_even()[0].start()
+
+    @pl.when(jump_is_odd)
+    def _():
+        jump_odd().start()
+        corner_odd()[0].start()
 
     row, other = grid(2 * ROWS, 2 * ROWS)
     way = jnp.where(even, 1, -1)
@@ -332,35 +375,50 @@
     def pass_on():
         @pl.when(jump_is_even)
         def _():
-            jump_even()[0].wait_recv()
+            jump_even().wait_recv()
             corner_odd()[1].wait_recv()
             pass_even().start()
 
         @pl.when(jump_is_odd)
         def _():
-            for copy in jump_odd():
-                copy.wait_recv()
+            jump_odd().wait_recv()
             corner_even()[1].wait_recv()
             pass_odd().start()
 
     def zonal_edges():
-        @pl.when(jump)
-        def _():
-            @pl.when(even)
-            def _():
-                corner_odd()[0].wait_recv()
-                pass_odd().wait_recv()
-
-            @pl.when(odd)
-            def _():
-                corner_even()[0].wait_recv()
-                pass_even().wait_recv()
-
-            to = jnp.where(high_jump, lons + half, 0)
+        day_of, slot = grid(3 * ROWS, 3 * ROWS)
+        held = jnp.where(even & (slot > DAY_HALF), slot - 1, slot)
+        spare = jnp.where(even, DAY_HALF, days)
+        away = jnp.abs(day_of - held)
+        edge_band = jnp.where(away <= DAY_HALF, -1.0, 0.0)
+        edge_band = jnp.where(away == 0, 2.0 * DAY_HALF, edge_band)
+        edge_band = jnp.where(slot == spare, 0.0, edge_band).astype(jnp.bfloat16)
+        to = jnp.where(high_jump, lons + half, 0)
+
+        @pl.when(jump_is_even)
+        def _():
+            corner_odd()[0].wait_recv()
+            pass_odd().wait_recv()
             for i in range(half):
                 anomaly[to + i] = (
-                    dot(own_band, edge_own[i])
+                    dot(edge_band, edge_own[i])
                     + dot(before_band, edge_before[i])
+                    + dot(after_band, edge_after[i])
+                )
+
+        @pl.when(jump_is_odd)
+        def _():
+            corner_even()[0].wait_recv()
+            pass_even().wait_recv()
+            day_of, slot = grid(3 * ROWS, 2 * ROWS)
+            held = jnp.where(slot > part, slot - 1, slot)
+            pass_band = jnp.where(
+                (held >= day_of) & (slot != part), -1.0, 0.0
+            ).astype(jnp.bfloat16)
+            for i in range(half):
+                anomaly[to + i] = (
+                    dot(edge_band, edge_own[i])
+                    + dot(pass_band, edge_pass[i])
                     + dot(after_band, edge_after[i])
                 )
 
@@ -441,12 +499,12 @@
 
     @pl.when(jump_is_even)
     def _():
-        for copy in (*jump_even(), *corner_even(), pass_even()):
+        for copy in (jump_even(), *corner_even(), pass_even()):
             copy.wait_send()
 
     @pl.when(jump_is_odd)
     def _():
-        for copy in (*jump_odd(), *corner_odd(), pass_odd()):
+        for copy in (jump_odd(), *corner_odd(), pass_odd()):
             copy.wait_send()
 
 
@@ -468,9 +526,11 @@
             pltpu.VMEM((lons, DAY_HALF, cols), jnp.bfloat16),
             pltpu.VMEM((lons, ROWS, cols), jnp.bfloat16),
             pltpu.VMEM((lons + 2 * half, 3 * ROWS, cols), jnp.float32),
-            pltpu.VMEM((half, days, cols), jnp.bfloat16),
+            pltpu.VMEM((half, 3 * ROWS, cols), jnp.bfloat16),
             pltpu.VMEM((half, DAY_HALF, cols), jnp.bfloat16),
             pltpu.VMEM((half, 2 * ROWS, cols), jnp.bfloat16),
+            pltpu.VMEM((half, 2 * ROWS, cols), jnp.bfloat16),
+            pltpu.VMEM((half, ROWS, cols), jnp.bfloat16),
             pltpu.SemaphoreType.DMA((lons // BLOCK,)),
             pltpu.SemaphoreType.DMA((2, steps)),
             pltpu.SemaphoreType.DMA((2, steps)),
@@ -481,6 +541,8 @@
             pltpu.SemaphoreType.DMA((8,)),
             pltpu.SemaphoreType.DMA((8,)),
             pltpu.SemaphoreType.REGULAR,
+            pltpu.SemaphoreType.REGULAR,
+            pltpu.SemaphoreType.REGULAR,
         ],
         compiler_params=pltpu.CompilerParams(
             collective_id=0, has_side_effects=True, vmem_limit_bytes=52 * 1024 * 1024

time: 83.7 us -> 73.2 us (0.87)
  Pallas kernels: 80.1 us -> 69.6 us
    pallas_call x1, Pallas kernels: 80.1 us -> 69.6 us  [local(): pl.pallas_call(functools.partial(kernel, counts), out_shape=pltpu.VMEM((l...]
where the time goes in v2:
time: 73.2 us
  Pallas kernels  69.6 us (95%)
  local copies, waits for them, and re-layouts  3.55 us (5%)
    pallas_call x1, Pallas kernels, local(): pl.pallas_call(functools.partial(kernel, counts), out_shape=pltpu.VMEM((l...  69.6 us
    unnamed x1, local copies, waits for them, and re-layouts  3.55 us

profile of v2, /device:TPU:1, one launch (start us, length us, event | category | flops | bytes accessed | tf_op | source)
XLA Modules:
  0.0 73.2 jit_solution(7650213194984679128)
XLA Ops:
  0.0 69.6 %shard_map.17 = f32[90,23,1024]{2,1,0:T(8,128)S(1)} custom-call(bf16[90,23,1024]{2,1,0:T(8,128)(2,1)} %bitcast.3), custom_call_target="tpu_custom_call" | custom-call | tf_op jit(solution)/shard_map/pallas_call | solution.py:517
  69.6 3.6 %copy.3 = f32[23,90,1024]{2,0,1:T(8,128)} copy(f32[23,90,1024]{2,0,1:T(8,128)S(1)} %bitcast.2) | data formatting | bytes 16957440

commit v3 on v2

--- a/solution.py
+++ b/solution.py
@@ -12,6 +12,7 @@
 ROWS = 8
 RUN = 8
 BLOCK = 10
+SHARE = 3
 MESH = pl.DeviceIdType.MESH
 
 
@@ -62,9 +63,10 @@
 
 def kernel(
     counts, x, out, own, far_days, after, before, packed, anomaly,
-    edge_own, edge_before, edge_after, edge_pass, edge_pack,
+    edge_own, edge_before, edge_after, edge_pass, edge_pack, relay,
     own_sem, far_send, far_recv, near_send, near_recv, lon_send, lon_recv,
     jump_send, jump_recv, near_ready, far_ready, lon_ready,
+    chain_ready, jump_ready,
 ):
     lons, days, cols = x.shape
     half = LON_HALF
@@ -78,8 +80,12 @@
     odd = jnp.logical_not(even)
     far = jnp.where(even, day_back, day_next)
     near = jnp.where(even, day_next, day_back)
-    low_jump = lax.rem(lon, RUN) == 0
-    high_jump = lax.rem(lon, RUN) == RUN - 1
+    zone = lax.rem(lon, RUN)
+    low = zone < RUN // 2
+    reach = jnp.where(low, zone, RUN - 1 - zone)
+    toward = jnp.where(low, lon_back, lon_next)
+    low_jump = zone == 0
+    high_jump = zone == RUN - 1
     jump = jnp.logical_or(low_jump, high_jump)
     peer = jnp.where(high_jump, lon_next, lon_back)
     edges, middle = plan(lons)
@@ -174,13 +180,25 @@
     across = {"lon": peer}
     corner = {"day": far, "lon": peer}
 
-    def jump_even():
-        return remote(edge_pack, edge_own.at[:, pl.ds(2 * ROWS, ROWS)],
+    row_of = pl.multiple_of(jnp.where(even, 2 * ROWS, 0), ROWS)
+    relays = RUN // 2 - 1
+    direct = half - relays * SHARE
+
+    def jump_direct():
+        rows = pl.ds(0, direct)
+        return remote(edge_pack.at[rows], edge_own.at[rows, pl.ds(row_of, ROWS)],
                       jump_send.at[0], jump_recv.at[0], across)
 
-    def jump_odd():
-        return remote(x.at[edge, pl.ds(0, ROWS)], edge_own.at[:, pl.ds(0, ROWS)],
-                      jump_send.at[0], jump_recv.at[0], across)
+    def jump_relay(r):
+        by = lax.rem(jnp.where(high_jump, lon + 1 + r, lon + lon_count - 1 - r), lon_count)
+        return remote(edge_pack.at[pl.ds(direct + (r - 1) * SHARE, SHARE)], relay,
+                      jump_send.at[7 + r], jump_recv.at[1], {"lon": by})
+
+    def relay_out(r):
+        rows = pl.ds(direct + (r - 1) * SHARE, SHARE)
+        return remote(relay, edge_own.at[rows, pl.ds(row_of, ROWS)],
+                      jump_send.at[1], jump_recv.at[7 + r],
+                      {"lon": jnp.where(low, lon - reach, lon + reach)})
 
     def corner_even():
         return [
@@ -264,9 +282,9 @@
     after_band = band(3 * ROWS, 2 * ROWS, days)
     second(len(order) - 1).start()
 
-    @pl.when(jump_is_even)
-    def _():
-        take = ones(col == DAY_HALF + place)
+    @pl.when(jump)
+    def _():
+        take = ones(col == jnp.where(even, DAY_HALF, 0) + place)
         for i in range(half):
             edge_pack[i] = dot(take, own[edge.start + i]).astype(jnp.bfloat16)
 
@@ -309,13 +327,29 @@
 
     @pl.when(jump_is_even)
     def _():
-        jump_even().start()
         corner_even()[0].start()
 
     @pl.when(jump_is_odd)
     def _():
-        jump_odd().start()
         corner_odd()[0].start()
+
+    @pl.when(reach == 2)
+    def _():
+        tell(chain_ready, "lon", toward)
+
+    @pl.when(reach == 1)
+    def _():
+        pl.semaphore_wait(chain_ready, 1)
+        tell(chain_ready, "lon", toward)
+
+    @pl.when(jump)
+    def _():
+        pl.semaphore_wait(chain_ready, 1)
+        tell(jump_ready, "lon", toward)
+        pl.semaphore_wait(jump_ready, 1)
+        jump_direct().start()
+        for r in range(1, relays + 1):
+            jump_relay(r).start()
 
     row, other = grid(2 * ROWS, 2 * ROWS)
     way = jnp.where(even, 1, -1)
@@ -345,11 +379,11 @@
 
     def shift(n):
         at, size = pieces[n]
-        low = n % 2 == 0
-        place = at + half + (lons if low else -lons)
+        down = n % 2 == 0
+        place = at + half + (lons if down else -lons)
         return remote(
             anomaly.at[pl.ds(at + half, size)], anomaly.at[pl.ds(place, size)],
-            lon_send.at[n], lon_recv.at[n], {"lon": lon_back if low else lon_next},
+            lon_send.at[n], lon_recv.at[n], {"lon": lon_back if down else lon_next},
         )
 
     def advance(n):
@@ -373,15 +407,19 @@
         corner_odd()[1].start()
 
     def pass_on():
+        @pl.when(jump)
+        def _():
+            jump_direct().wait_recv()
+            for r in range(1, relays + 1):
+                relay_out(r).wait_recv()
+
         @pl.when(jump_is_even)
         def _():
-            jump_even().wait_recv()
             corner_odd()[1].wait_recv()
             pass_even().start()
 
         @pl.when(jump_is_odd)
         def _():
-            jump_odd().wait_recv()
             corner_even()[1].wait_recv()
             pass_odd().start()
 
@@ -454,9 +492,14 @@
     done = half
     for n in range(len(edges), steps):
         end = n == steps - 1
-        if n == steps - 3:
+        if n == steps - 5:
+            @pl.when(reach > 0)
+            def _():
+                jump_relay(1).wait_recv()
+                relay_out(reach).start()
+        if n == steps - 4:
             pass_on()
-        if end:
+        if n == steps - 2:
             zonal_edges()
             lax.fori_loop(0, half, back, first_total)
         advance(n)
@@ -497,14 +540,24 @@
         def _():
             shift(n).wait_send()
 
+    @pl.when(jump)
+    def _():
+        jump_direct().wait_send()
+        for r in range(1, relays + 1):
+            jump_relay(r).wait_send()
+
+    @pl.when(reach > 0)
+    def _():
+        relay_out(reach).wait_send()
+
     @pl.when(jump_is_even)
     def _():
-        for copy in (jump_even(), *corner_even(), pass_even()):
+        for copy in (*corner_even(), pass_even()):
             copy.wait_send()
 
     @pl.when(jump_is_odd)
     def _():
-        for copy in (jump_odd(), *corner_odd(), pass_odd()):
+        for copy in (*corner_odd(), pass_odd()):
             copy.wait_send()
 
 
@@ -531,6 +584,7 @@
             pltpu.VMEM((half, 2 * ROWS, cols), jnp.bfloat16),
             pltpu.VMEM((half, 2 * ROWS, cols), jnp.bfloat16),
             pltpu.VMEM((half, ROWS, cols), jnp.bfloat16),
+            pltpu.VMEM((SHARE, ROWS, cols), jnp.bfloat16),
             pltpu.SemaphoreType.DMA((lons // BLOCK,)),
             pltpu.SemaphoreType.DMA((2, steps)),
             pltpu.SemaphoreType.DMA((2, steps)),
@@ -538,8 +592,10 @@
             pltpu.SemaphoreType.DMA((lons // BLOCK,)),
             pltpu.SemaphoreType.DMA((4,)),
             pltpu.SemaphoreType.DMA((4,)),
-            pltpu.SemaphoreType.DMA((8,)),
-            pltpu.SemaphoreType.DMA((8,)),
+            pltpu.SemaphoreType.DMA((11,)),
+            pltpu.SemaphoreType.DMA((11,)),
+            pltpu.SemaphoreType.REGULAR,
+            pltpu.SemaphoreType.REGULAR,
             pltpu.SemaphoreType.REGULAR,
             pltpu.SemaphoreType.REGULAR,
             pltpu.SemaphoreType.REGULAR,

time: 73.2 us -> 69.5 us (0.949)
  Pallas kernels: 69.6 us -> 65.7 us
    pallas_call x1, Pallas kernels: 69.6 us -> 65.7 us  [local(): pl.pallas_call(functools.partial(kernel, counts), out_shape=pltpu.VMEM((l...]
where the time goes in v3:
time: 69.5 us; the launch traced here: 69.3 us
  Pallas kernels  65.7 us (95%)
  local copies, waits for them, and re-layouts  3.55 us (5%)
    pallas_call x1, Pallas kernels, local(): pl.pallas_call(functools.partial(kernel, counts), out_shape=pltpu.VMEM((l...  65.7 us
    unnamed x1, local copies, waits for them, and re-layouts  3.55 us

profile of v3, /device:TPU:1, one launch (start us, length us, event | category | flops | bytes accessed | tf_op | source)
XLA Modules:
  0.0 69.3 jit_solution(14738216223098009306)
XLA Ops:
  0.0 65.7 %shard_map.17 = f32[90,23,1024]{2,1,0:T(8,128)S(1)} custom-call(bf16[90,23,1024]{2,1,0:T(8,128)(2,1)} %bitcast.3), custom_call_target="tpu_custom_call" | custom-call | tf_op jit(solution)/shard_map/pallas_call | solution.py:570
  65.7 3.6 %copy.3 = f32[23,90,1024]{2,0,1:T(8,128)} copy(f32[23,90,1024]{2,0,1:T(8,128)S(1)} %bitcast.2) | data formatting | bytes 16957440

commit v4 on v3

--- a/solution.py
+++ b/solution.py
@@ -62,7 +62,7 @@
 
 
 def kernel(
-    counts, x, out, own, far_days, after, before, packed, anomaly,
+    counts, x, out, anomaly, own, far_days, after, before, packed,
     edge_own, edge_before, edge_after, edge_pass, edge_pack, relay,
     own_sem, far_send, far_recv, near_send, near_recv, lon_send, lon_recv,
     jump_send, jump_recv, near_ready, far_ready, lon_ready,
@@ -102,7 +102,7 @@
 
     barrier = pltpu.get_barrier_semaphore()
     seat = lax.rem(day, 4)
-    hub = seat == 1
+    hub = seat == 0
     rest = jnp.logical_not(hub)
 
     def tell(semaphore, axis, *peers):
@@ -111,29 +111,29 @@
                 semaphore, inc=1, device_id={axis: who}, device_id_type=MESH
             )
 
-    @pl.when(jnp.logical_or(hub, seat == 3))
+    @pl.when(jnp.logical_or(hub, seat == 2))
     def _():
         tell(barrier, "day", day_back, day_next)
 
-    @pl.when(seat == 0)
+    @pl.when(seat == 1)
+    def _():
+        tell(barrier, "day", day_next)
+
+    @pl.when(seat == 3)
     def _():
         tell(barrier, "day", day_back)
 
-    @pl.when(seat == 2)
-    def _():
-        tell(barrier, "day", day_next)
-
     @pl.when(rest)
     def _():
         pl.semaphore_wait(barrier, 2)
 
-    @pl.when(seat == 0)
-    def _():
-        tell(near_ready, "day", day_next)
-
-    @pl.when(seat == 2)
-    def _():
-        tell(far_ready, "day", day_back)
+    @pl.when(seat == 1)
+    def _():
+        tell(near_ready, "day", day_back)
+
+    @pl.when(seat == 3)
+    def _():
+        tell(far_ready, "day", day_next)
 
     @pl.when(hub)
     def _():
@@ -151,7 +151,7 @@
         at, size, _ = order[n]
         rows = pl.ds(at, size)
         return remote(
-            x.at[rows, pl.ds(start, ROWS)], far_days.at[rows, pl.ds(0, ROWS)],
+            (own if n else x).at[rows, pl.ds(start, ROWS)], far_days.at[rows, pl.ds(0, ROWS)],
             far_send.at[0, n], far_recv.at[0, n], {"day": far},
         )
 
@@ -227,7 +227,16 @@
     jump_is_even = jnp.logical_and(jump, even)
     jump_is_odd = jnp.logical_and(jump, odd)
 
+    waited = [0]
+
+    def loaded(count):
+        while waited[0] < count:
+            load(sequence[waited[0]]).wait()
+            waited[0] += 1
+
     for n in range(len(edges)):
+        if n:
+            loaded(n + 1)
         whole(n).start()
 
     @pl.when(hub)
@@ -260,23 +269,17 @@
                 tile = tile + dot(ride, own[rider])
             packed[at + i] = tile.astype(jnp.bfloat16)
 
-    waited = 0
     for n in range(len(order)):
         at, size, _ = order[n]
-        need = 2 if n < 2 else 4 if n < 4 else min(
-            blocks, max(4, sequence.index(min((at + size - 1) // BLOCK, blocks - 3)) + 1)
-        )
-        while waited < need:
-            load(sequence[waited]).wait()
-            waited += 1
+        if n >= len(edges):
+            last = min((at + size - 1) // BLOCK, blocks - 3)
+            loaded(max(4, sequence.index(last) + 1))
         if n >= len(edges):
             whole(n).start()
         pack(n)
         if n > 0:
             second(n - 1).start()
-    while waited < blocks:
-        load(sequence[waited]).wait()
-        waited += 1
+    loaded(blocks)
     own_band = band(3 * ROWS, days, 0)
     before_band = band(3 * ROWS, DAY_HALF, -DAY_HALF)
     after_band = band(3 * ROWS, 2 * ROWS, days)
@@ -311,17 +314,17 @@
         pl.semaphore_wait(barrier, 2)
         tell(lon_ready, "day", day_back, day_next)
 
-    @pl.when(seat == 0)
+    @pl.when(seat == 1)
+    def _():
+        pl.semaphore_wait(lon_ready, 1)
+        tell(lon_ready, "day", day_next)
+
+    @pl.when(seat == 3)
     def _():
         pl.semaphore_wait(lon_ready, 1)
         tell(lon_ready, "day", day_back)
 
     @pl.when(seat == 2)
-    def _():
-        pl.semaphore_wait(lon_ready, 1)
-        tell(lon_ready, "day", day_next)
-
-    @pl.when(seat == 3)
     def _():
         pl.semaphore_wait(lon_ready, 2)
 
@@ -503,8 +506,8 @@
             zonal_edges()
             lax.fori_loop(0, half, back, first_total)
         advance(n)
-        ready = lons if end else order[n][0] + order[n][1] - half
-        if ready <= half:
+        ready = order[n][0] + order[n][1] - half
+        if ready <= half or end:
             continue
         if total is None:
             total = lax.fori_loop(
@@ -561,24 +564,68 @@
             copy.wait_send()
 
 
+def store(held, anomaly, out, last, done):
+    split, days, _ = held.shape
+    count = last.shape[0]
+    half = LON_HALF
+    width = 2 * half + 1
+    scale = 1.0 / ((2 * DAY_HALF + 1) * width)
+    copies = []
+
+    def copy(source, at, to, size):
+        copies.append(
+            pltpu.make_async_copy(
+                source.at[pl.ds(at, size)], out.at[pl.ds(to, size)], done.at[len(copies)]
+            )
+        )
+        copies[-1].start()
+
+    for at in range(0, split, BLOCK):
+        copy(held, at, at, min(BLOCK, split - at))
+
+    def step(l, total):
+        total = total + (anomaly[split + l + width - 1] - anomaly[split + l - 1])
+        last[l] = (total * scale)[:days]
+        return total
+
+    total = lax.fori_loop(
+        split - 1,
+        split - 1 + width,
+        lambda l, t: t + anomaly[l],
+        jnp.zeros(anomaly.shape[1:], jnp.float32),
+    )
+    for at in range(0, count, BLOCK):
+        size = min(BLOCK, count - at)
+        total = lax.fori_loop(at, at + size, step, total)
+        copy(last, at, split + at, size)
+    for started in copies:
+        started.wait()
+
+
 def local(counts, field):
     days, lons, cols = field.shape
     x = jnp.transpose(field, (1, 0, 2))
     edges, middle = plan(lons)
     steps = len(edges) + len(middle)
     half = LON_HALF
-    y = pl.pallas_call(
+    split = middle[-1][0] - half
+    held, anomaly = pl.pallas_call(
         functools.partial(kernel, counts),
-        out_shape=pltpu.VMEM((lons, days, cols), jnp.float32),
+        out_shape=(
+            pltpu.VMEM((split, days, cols), jnp.float32),
+            pltpu.VMEM((lons + 2 * half, 3 * ROWS, cols), jnp.float32),
+        ),
         in_specs=[pl.BlockSpec(memory_space=pltpu.HBM)],
-        out_specs=pl.BlockSpec(memory_space=pltpu.VMEM),
+        out_specs=(
+            pl.BlockSpec(memory_space=pltpu.VMEM),
+            pl.BlockSpec(memory_space=pltpu.VMEM),
+        ),
         scratch_shapes=[
             pltpu.VMEM((lons, days, cols), jnp.bfloat16),
             pltpu.VMEM((lons, 2 * ROWS, cols), jnp.bfloat16),
             pltpu.VMEM((lons, 2 * ROWS, cols), jnp.bfloat16),
             pltpu.VMEM((lons, DAY_HALF, cols), jnp.bfloat16),
             pltpu.VMEM((lons, ROWS, cols), jnp.bfloat16),
-            pltpu.VMEM((lons + 2 * half, 3 * ROWS, cols), jnp.float32),
             pltpu.VMEM((half, 3 * ROWS, cols), jnp.bfloat16),
             pltpu.VMEM((half, DAY_HALF, cols), jnp.bfloat16),
             pltpu.VMEM((half, 2 * ROWS, cols), jnp.bfloat16),
@@ -601,10 +648,25 @@
             pltpu.SemaphoreType.REGULAR,
         ],
         compiler_params=pltpu.CompilerParams(
-            collective_id=0, has_side_effects=True, vmem_limit_bytes=52 * 1024 * 1024
+            collective_id=0, has_side_effects=True, vmem_limit_bytes=44 * 1024 * 1024
         ),
     )(x)
-    return jnp.transpose(y, (1, 0, 2))
+    count = lons - split
+    z = pl.pallas_call(
+        store,
+        out_shape=pltpu.HBM((lons, days, cols), jnp.float32),
+        in_specs=[pl.BlockSpec(memory_space=pltpu.VMEM)] * 2,
+        out_specs=pl.BlockSpec(memory_space=pltpu.HBM),
+        scratch_shapes=[
+            pltpu.VMEM((count, days, cols), jnp.float32),
+            pltpu.SemaphoreType.DMA((-(-split // BLOCK) - (-count // BLOCK),)),
+        ],
+        compiler_params=pltpu.CompilerParams(vmem_limit_bytes=8 * 1024 * 1024),
+    )(
+        pltpu.with_memory_space_constraint(held, pltpu.VMEM),
+        pltpu.with_memory_space_constraint(anomaly, pltpu.VMEM),
+    )
+    return jnp.transpose(z, (1, 0, 2))
 
 
 def solution(mesh):

time: 69.5 us -> 68.8 us (0.990)
  local copies, waits for them, and re-layouts: 3.55 us -> 0 us
  Pallas kernels: 65.7 us -> 68.7 us
    unnamed x1 -> x0, local copies, waits for them, and re-layouts: 3.55 us -> none
    pallas_call x1 -> x2, Pallas kernels: 65.7 us -> 68.7 us  [the longest x1 65.2 us: local(): pl.pallas_call(functools.partial(kernel, counts), out_shape=(pltpu.VMEM((...]
where the time goes in v4:
time: 68.8 us; the launch traced here: 68.7 us
  Pallas kernels  68.7 us (100%)
    pallas_call x1, Pallas kernels, local(): pl.pallas_call(functools.partial(kernel, counts), out_shape=(pltpu.VMEM((...  65.2 us
    pallas_call x1, Pallas kernels, local(): pl.pallas_call(store, out_shape=pltpu.HBM((lons, days, cols), jnp.float32...  3.53 us

profile of v4, /device:TPU:1, one launch (start us, length us, event | category | flops | bytes accessed | tf_op | source)
XLA Modules:
  0.0 68.7 jit_solution(11552188069740935099)
XLA Ops:
  0.0 65.2 %shard_map.17 = (f32[62,23,1024]{2,1,0:T(8,128)S(1)}, f32[110,24,1024]{2,1,0:T(8,128)S(1)}) custom-call(bf16[90,23,1024]{2,1,0:T(8,128)(2,1)} %bitcast.2), custom_call_target="tpu_custom_call" | custom-call | tf_op jit(solution)/shard_map/pallas_call | solution.py:612
  65.2 3.5 %shard_map.18 = f32[90,23,1024]{2,1,0:T(8,128)} custom-call(f32[62,23,1024]{2,1,0:T(8,128)S(1)} %get-tuple-element.7.held, f32[110,24,1024]{2,1,0:T(8,128)S(1)} %get-tuple-element.8.anomaly), custom_call_target="tpu_custom_call" | custom-call | tf_op jit(solution)/shard_map/pallas_call | solution.py:655

commit v5 on v4

--- a/solution.py
+++ b/solution.py
@@ -62,7 +62,7 @@
 
 
 def kernel(
-    counts, x, out, anomaly, own, far_days, after, before, packed,
+    counts, x, out, anomaly, far_days, own, after, before, packed,
     edge_own, edge_before, edge_after, edge_pass, edge_pack, relay,
     own_sem, far_send, far_recv, near_send, near_recv, lon_send, lon_recv,
     jump_send, jump_recv, near_ready, far_ready, lon_ready,
@@ -399,6 +399,11 @@
                 shift(n - 1).start()
 
     for n in range(len(edges)):
+        if n == 2:
+            @pl.when(reach > 0)
+            def _():
+                jump_relay(1).wait_recv()
+                relay_out(reach).start()
         advance(n)
 
     @pl.when(jump_is_even)
@@ -490,24 +495,28 @@
         out[l] = (total * scale)[:days]
         return total
 
+    def finish_edges(total):
+        zonal_edges()
+        lax.fori_loop(0, half, back, total)
+
+    early = jnp.logical_or(seat == 0, seat == 3)
+    late = jnp.logical_not(early)
     steps = len(order)
     total = None
     done = half
     for n in range(len(edges), steps):
         end = n == steps - 1
-        if n == steps - 5:
-            @pl.when(reach > 0)
-            def _():
-                jump_relay(1).wait_recv()
-                relay_out(reach).start()
         if n == steps - 4:
-            pass_on()
+            pl.when(late)(pass_on)
         if n == steps - 2:
-            zonal_edges()
-            lax.fori_loop(0, half, back, first_total)
+            pl.when(late)(functools.partial(finish_edges, first_total))
+        if end:
+            whole(n).wait_recv()
+            second(n).wait_recv()
+            continue
         advance(n)
         ready = order[n][0] + order[n][1] - half
-        if ready <= half or end:
+        if ready <= half:
             continue
         if total is None:
             total = lax.fori_loop(
@@ -522,6 +531,11 @@
         total = up_to(done, ready, total)
         done = ready
 
+    @pl.when(early)
+    def _():
+        pass_on()
+        finish_edges(first_total)
+
     for n in range(steps):
         whole(n).wait_send()
         second(n).wait_send()
@@ -564,7 +578,7 @@
             copy.wait_send()
 
 
-def store(held, anomaly, out, last, done):
+def store(final, late, held, anomaly, far_days, out, last, part, done):
     split, days, _ = held.shape
     count = last.shape[0]
     half = LON_HALF
@@ -583,6 +597,14 @@
     for at in range(0, split, BLOCK):
         copy(held, at, at, min(BLOCK, split - at))
 
+    day, other = grid(3 * ROWS, 2 * ROWS)
+    even = lax.rem(lax.axis_index("day"), 2) == 0
+    first = jnp.where(even, day - other, other - day + ROWS)
+    far_band = jnp.where((first <= 0) & (other < DAY_HALF), -1.0, 0.0)
+    far_band = far_band.astype(jnp.bfloat16)
+    for i in range(late):
+        part[i] = dot(far_band, far_days[final + i])
+
     def step(l, total):
         total = total + (anomaly[split + l + width - 1] - anomaly[split + l - 1])
         last[l] = (total * scale)[:days]
@@ -594,10 +616,20 @@
         lambda l, t: t + anomaly[l],
         jnp.zeros(anomaly.shape[1:], jnp.float32),
     )
-    for at in range(0, count, BLOCK):
-        size = min(BLOCK, count - at)
-        total = lax.fori_loop(at, at + size, step, total)
-        copy(last, at, split + at, size)
+    done_to, sent = 0, 0
+    for at, sign in sorted(
+        [(i, 1) for i in range(late)]
+        + [(width + i, -1) for i in range(late)]
+        + [(count, 0)]
+    ):
+        total = lax.fori_loop(done_to, at, step, total)
+        if sign:
+            fresh = part[at] if sign > 0 else -part[at - width]
+            total = step(at, total + fresh)
+            done_to = at + 1
+        if sent + BLOCK <= at or at == count:
+            copy(last, sent, split + sent, at - sent)
+            sent = at
     for started in copies:
         started.wait()
 
@@ -609,20 +641,17 @@
     steps = len(edges) + len(middle)
     half = LON_HALF
     split = middle[-1][0] - half
-    held, anomaly = pl.pallas_call(
+    held, anomaly, far_days = pl.pallas_call(
         functools.partial(kernel, counts),
         out_shape=(
             pltpu.VMEM((split, days, cols), jnp.float32),
             pltpu.VMEM((lons + 2 * half, 3 * ROWS, cols), jnp.float32),
+            pltpu.VMEM((lons, 2 * ROWS, cols), jnp.bfloat16),
         ),
         in_specs=[pl.BlockSpec(memory_space=pltpu.HBM)],
-        out_specs=(
-            pl.BlockSpec(memory_space=pltpu.VMEM),
-            pl.BlockSpec(memory_space=pltpu.VMEM),
-        ),
+        out_specs=(pl.BlockSpec(memory_space=pltpu.VMEM),) * 3,
         scratch_shapes=[
             pltpu.VMEM((lons, days, cols), jnp.bfloat16),
-            pltpu.VMEM((lons, 2 * ROWS, cols), jnp.bfloat16),
             pltpu.VMEM((lons, 2 * ROWS, cols), jnp.bfloat16),
             pltpu.VMEM((lons, DAY_HALF, cols), jnp.bfloat16),
             pltpu.VMEM((lons, ROWS, cols), jnp.bfloat16),
@@ -648,23 +677,25 @@
             pltpu.SemaphoreType.REGULAR,
         ],
         compiler_params=pltpu.CompilerParams(
-            collective_id=0, has_side_effects=True, vmem_limit_bytes=44 * 1024 * 1024
+            collective_id=0, has_side_effects=True, vmem_limit_bytes=40 * 1024 * 1024
         ),
     )(x)
     count = lons - split
     z = pl.pallas_call(
-        store,
+        functools.partial(store, *middle[-1][:2]),
         out_shape=pltpu.HBM((lons, days, cols), jnp.float32),
-        in_specs=[pl.BlockSpec(memory_space=pltpu.VMEM)] * 2,
+        in_specs=[pl.BlockSpec(memory_space=pltpu.VMEM)] * 3,
         out_specs=pl.BlockSpec(memory_space=pltpu.HBM),
         scratch_shapes=[
             pltpu.VMEM((count, days, cols), jnp.float32),
+            pltpu.VMEM((middle[-1][1], 3 * ROWS, cols), jnp.float32),
             pltpu.SemaphoreType.DMA((-(-split // BLOCK) - (-count // BLOCK),)),
         ],
         compiler_params=pltpu.CompilerParams(vmem_limit_bytes=8 * 1024 * 1024),
     )(
         pltpu.with_memory_space_constraint(held, pltpu.VMEM),
         pltpu.with_memory_space_constraint(anomaly, pltpu.VMEM),
+        pltpu.with_memory_space_constraint(far_days, pltpu.VMEM),
     )
     return jnp.transpose(z, (1, 0, 2))
 

time: 68.8 us -> 68.7 us (level)
  no operation moved by 1% of the time
where the time goes in v5:
time: 68.7 us; the launch traced here: 68.6 us
  Pallas kernels  68.6 us (100%)
    pallas_call x1, Pallas kernels, local(): pl.pallas_call(functools.partial(kernel, counts), out_shape=(pltpu.VMEM((...  65 us
    pallas_call x1, Pallas kernels, local(): pl.pallas_call(functools.partial(store, *middle[-1][:2]), out_shape=pltpu...  3.54 us

profile of v5, /device:TPU:1, one launch (start us, length us, event | category | flops | bytes accessed | tf_op | source)
XLA Modules:
  0.0 68.6 jit_solution(12995655595594526536)
XLA Ops:
  0.0 65.0 %shard_map.17 = (f32[62,23,1024]{2,1,0:T(8,128)S(1)}, f32[110,24,1024]{2,1,0:T(8,128)S(1)}, bf16[90,16,1024]{2,1,0:T(8,128)(2,1)S(1)}) custom-call(bf16[90,23,1024]{2,1,0:T(8,128)(2,1)} %bitcast.2), custom_call_target="tpu_custom_call" | custom-call | tf_op jit(solution)/shard_map/pallas_call | solution.py:644
  65.1 3.5 %shard_map.18 = f32[90,23,1024]{2,1,0:T(8,128)} custom-call(f32[62,23,1024]{2,1,0:T(8,128)S(1)} %get-tuple-element.8.held, f32[110,24,1024]{2,1,0:T(8,128)S(1)} %get-tuple-element.9.anomaly, bf16[90,16,1024]{2,1,0:T(8,128)(2,1)S(1)} %get-tuple-element.10.far_days), custom_call_target="tpu_custom_call" | custom-call | tf_op jit(solution)/shard_map/pallas_call | solution.py:684

commit v6 on v5

--- a/solution.py
+++ b/solution.py
@@ -147,11 +147,11 @@
 
     start = pl.multiple_of(jnp.where(even, 0, ROWS), ROWS)
 
-    def whole(n):
+    def whole(n, days_of=own):
         at, size, _ = order[n]
         rows = pl.ds(at, size)
         return remote(
-            (own if n else x).at[rows, pl.ds(start, ROWS)], far_days.at[rows, pl.ds(0, ROWS)],
+            days_of.at[rows, pl.ds(start, ROWS)], far_days.at[rows, pl.ds(0, ROWS)],
             far_send.at[0, n], far_recv.at[0, n], {"day": far},
         )
 
@@ -227,6 +227,11 @@
     jump_is_even = jnp.logical_and(jump, even)
     jump_is_odd = jnp.logical_and(jump, odd)
 
+    @pl.when(seat == 2)
+    def _():
+        for n in range(len(edges)):
+            whole(n, x).start()
+
     waited = [0]
 
     def loaded(count):
@@ -235,9 +240,11 @@
             waited[0] += 1
 
     for n in range(len(edges)):
-        if n:
-            loaded(n + 1)
-        whole(n).start()
+        loaded(n + 1)
+
+        @pl.when(seat != 2)
+        def _():
+            whole(n).start()
 
     @pl.when(hub)
     def _():

time: 68.7 us -> 68.7 us (level)
  no operation moved by 1% of the time
where the time goes in v6:
time: 68.7 us; the launch traced here: 68.6 us
  Pallas kernels  68.6 us (100%)
    pallas_call x1, Pallas kernels, local(): pl.pallas_call(functools.partial(kernel, counts), out_shape=(pltpu.VMEM((...  65 us
    pallas_call x1, Pallas kernels, local(): pl.pallas_call(functools.partial(store, *middle[-1][:2]), out_shape=pltpu...  3.54 us

profile of v6, /device:TPU:1, one launch (start us, length us, event | category | flops | bytes accessed | tf_op | source)
XLA Modules:
  0.0 68.6 jit_solution(4590586426918826295)
XLA Ops:
  0.0 65.0 %shard_map.17 = (f32[62,23,1024]{2,1,0:T(8,128)S(1)}, f32[110,24,1024]{2,1,0:T(8,128)S(1)}, bf16[90,16,1024]{2,1,0:T(8,128)(2,1)S(1)}) custom-call(bf16[90,23,1024]{2,1,0:T(8,128)(2,1)} %bitcast.2), custom_call_target="tpu_custom_call" | custom-call | tf_op jit(solution)/shard_map/pallas_call | solution.py:651
  65.1 3.5 %shard_map.18 = f32[90,23,1024]{2,1,0:T(8,128)} custom-call(f32[62,23,1024]{2,1,0:T(8,128)S(1)} %get-tuple-element.8.held, f32[110,24,1024]{2,1,0:T(8,128)S(1)} %get-tuple-element.9.anomaly, bf16[90,16,1024]{2,1,0:T(8,128)(2,1)S(1)} %get-tuple-element.10.far_days), custom_call_target="tpu_custom_call" | custom-call | tf_op jit(solution)/shard_map/pallas_call | solution.py:691
